TPU v7x, 32 devices: a whole 2x2x4 slice. The times are simulated.
32 devices in a mesh: row: 8 (over z, core), col: 4 (over y, x).
Axes of the slice: x: 2, y: 2, z: 4, core: 2. Of those that a mesh axis runs over, the one named last changes fastest.
Arguments:
- substrate: float32 [1024, 1024], P('row', 'col'), may hold values from 0.05 to 0.95
- activator: float32 [1024, 1024], P('row', 'col'), may hold values from 0 to 0.45
Outputs:
- substrate_section: float32 [1024, 1024], P('row', 'col')
- activator_section: float32 [1024, 1024], P('row', 'col')
All inputs are finite; a program needn't handle non-finite values.
Results may differ from a plain program's by a relative error of at most 0.00023.
Values sent between devices are 32-bit elements; how exact they have to be, the bound alone decides.
A program may use at most 64 MiB of HBM per device.

v0:
```python
import functools
import math

import jax
import jax.numpy as jnp
import numpy as np
from jax import lax
from jax.experimental import pallas as pl
from jax.experimental.pallas import tpu as pltpu
from jax.sharding import PartitionSpec as P

FEED_RATE = 0.037
KILL_RATE = 0.06
TIME_STEP = 8.0
SUBSTRATE_DIFFUSION = 4e-07
ACTIVATOR_DIFFUSION = 2e-07


def rotation(left_index, right_index, period, direction):
    phase_index = left_index * right_index % period
    angles = phase_index.astype(jnp.float32) * (2.0 * math.pi / period)
    return (jnp.cos(angles), direction * jnp.sin(angles))


def complex_matrix(size_count, direction):
    indices = jnp.arange(size_count, dtype=jnp.int32)
    cosine_part, sine_part = rotation(indices[:, None], indices[None, :], size_count, direction)
    return jnp.stack([jnp.stack([cosine_part, -sine_part]), jnp.stack([sine_part, cosine_part])])


def transform_last(values, direction):
    part_count, species, middle, length = values.shape
    leading = 64
    second = length // leading
    shaped = values.reshape(part_count, species, middle, leading, second)
    first_matrix = complex_matrix(leading, direction)
    first_pass = jnp.einsum(
        "pqka,qsmab->psmkb", first_matrix, shaped, precision=lax.Precision.HIGHEST
    )
    cosine_part, sine_part = rotation(
        jnp.arange(leading, dtype=jnp.int32)[:, None],
        jnp.arange(second, dtype=jnp.int32)[None, :],
        length,
        direction,
    )
    turned = jnp.stack(
        [
            first_pass[0] * cosine_part - first_pass[1] * sine_part,
            first_pass[0] * sine_part + first_pass[1] * cosine_part,
        ]
    )
    second_matrix = complex_matrix(second, direction)
    second_pass = jnp.einsum(
        "pqkb,qsmjb->psmkj", second_matrix, turned, precision=lax.Precision.HIGHEST
    )
    return second_pass.reshape(part_count, species, middle, length)


def signed_squares(wave_index, total):
    signed = jnp.where(2 * wave_index < total, wave_index, wave_index - total).astype(jnp.float32)
    angular = 2.0 * math.pi * signed
    return angular * angular


def section_factors(row_wave, col_wave, total_rows, total_cols):
    wave_number = signed_squares(row_wave, total_rows) + signed_squares(col_wave, total_cols)
    normalize = 1.0 / (total_rows * total_cols)
    growths = []
    forcings = []
    for diffusion, decay_rate in (
        (SUBSTRATE_DIFFUSION, FEED_RATE),
        (ACTIVATOR_DIFFUSION, FEED_RATE + KILL_RATE),
    ):
        linear = -diffusion * wave_number - decay_rate
        exponent = linear * (0.5 * TIME_STEP)
        growths.append(jnp.exp(exponent) * normalize)
        forcings.append(jnp.expm1(exponent) / linear * normalize)
    return (jnp.stack(growths), jnp.stack(forcings))


def advance(spectra, growth, forcing):
    real_part = spectra[0]
    imag_part = spectra[1]
    return jnp.stack(
        [growth * real_part + forcing * imag_part, growth * imag_part - forcing * real_part]
    )


def col_forward(values):
    return lax.all_to_all(values, "col", split_axis=2, concat_axis=3, tiled=True)


def col_backward(values):
    return lax.all_to_all(values, "col", split_axis=3, concat_axis=2, tiled=True)


def row_forward(values):
    return lax.all_to_all(values, "row", split_axis=2, concat_axis=3, tiled=True)


def row_backward(values):
    return lax.all_to_all(values, "row", split_axis=3, concat_axis=2, tiled=True)


def on_device(substrate, activator):
    row_count, col_count = substrate.shape
    total_rows = row_count * lax.axis_size("row")
    total_cols = col_count * lax.axis_size("col")
    row_index = lax.axis_index("row")
    col_index = lax.axis_index("col")
    reaction = substrate * activator * activator
    fields = jnp.stack(
        [jnp.stack([substrate, activator]), jnp.stack([FEED_RATE - reaction, reaction])]
    )
    spectra = transform_last(col_forward(fields), -1)
    spectra = row_forward(col_forward(jnp.swapaxes(spectra, 2, 3)))
    spectra = transform_last(spectra, -1)
    local_cols = col_count // lax.axis_size("row")
    col_wave = (
        col_count * col_index
        + local_cols * row_index
        + jnp.arange(local_cols, dtype=jnp.int32)[:, None]
    )
    row_wave = jnp.arange(total_rows, dtype=jnp.int32)[None, :]
    growth, forcing = section_factors(row_wave, col_wave, total_rows, total_cols)
    spectra = transform_last(advance(spectra, growth, forcing), 1)
    spectra = col_backward(row_backward(spectra))
    spectra = jnp.swapaxes(spectra, 2, 3)
    spectra = transform_last(spectra, 1)
    fields = lax.all_to_all(spectra[:1], "col", split_axis=3, concat_axis=2, tiled=True)
    return (fields[0, 0], fields[0, 1])


MESH = pl.DeviceIdType.MESH
LANES = 128


def split(values):
    high = values.astype(jnp.bfloat16)
    low = (values - high.astype(jnp.float32)).astype(jnp.bfloat16)
    return high, low


def contract_last(left, right):
    return lax.dot_general(
        left, right, (((1,), (1,)), ((), ())), preferred_element_type=jnp.float32
    )


def block_transpose(pieces):
    first, second, third, fourth = pieces
    lane = lax.broadcasted_iota(jnp.int32, first.shape, 1)
    upper = lane < LANES // 2
    even = lane // (LANES // 4) % 2 == 0

    def far(a, b):
        return (
            jnp.where(upper, a, pltpu.roll(b, LANES // 2, 1)),
            jnp.where(upper, pltpu.roll(a, LANES // 2, 1), b),
        )

    def near(a, b):
        return (
            jnp.where(even, a, pltpu.roll(b, LANES // 4, 1)),
            jnp.where(even, pltpu.roll(a, 3 * LANES // 4, 1), b),
        )

    first, third = far(first, third)
    second, fourth = far(second, fourth)
    first, second = near(first, second)
    third, fourth = near(third, fourth)
    return first, second, third, fourth


def section_kernel(
    rows, cols, u_hbm, v_hbm, tables_hbm, out_u, out_v, u_ref, v_ref, tables_ref,
    c_high, c_low, x_in, packed, wide, send, recv, result,
    ready, load_sem, in_send, in_recv, s_send, s_recv, out_send, out_recv,
):
    devices = rows * cols
    total = u_ref.shape[1] * cols
    band = u_ref.shape[0] // cols
    width = u_ref.shape[1]
    chunk = 256
    row = lax.axis_index("row")
    col = lax.axis_index("col")
    me = row * cols + col

    loads = [
        pltpu.make_async_copy(source, target, load_sem.at[index])
        for index, (source, target) in enumerate(
            ((u_hbm, u_ref), (v_hbm, v_ref), (tables_hbm, tables_ref))
        )
    ]
    for load in loads:
        load.start()
    barrier = pltpu.get_barrier_semaphore()

    def greet(semaphore, other_row, other_col):
        pl.semaphore_signal(
            semaphore, inc=1, device_id=(other_row, other_col), device_id_type=MESH
        )

    for step in range(1, cols):
        greet(barrier, row, lax.rem(col + step, cols))
    for step in range(1, rows):
        greet(barrier, lax.rem(row + step, rows), col)
    for load in loads[:2]:
        load.wait()
    pl.semaphore_wait(barrier, rows + cols - 2)

    def in_copy(step, field):
        ref = (u_ref, v_ref)[field]
        other = lax.rem(col + step, cols)
        return pltpu.make_async_remote_copy(
            src_ref=ref.at[pl.ds(pl.multiple_of(other * band, band), band)],
            dst_ref=x_in.at[field, col],
            send_sem=in_send.at[field, step],
            recv_sem=in_recv.at[field, step],
            device_id=(row, other),
            device_id_type=MESH,
        )

    in_copies = [[in_copy(step, field) for step in range(1, cols)] for field in range(2)]
    for copy in in_copies[1] + in_copies[0]:
        copy.start()
    for step in range(1, rows):
        greet(ready, lax.rem(row + step, rows), col)
    for field, ref in enumerate((u_ref, v_ref)):
        x_in[field, col] = ref[pl.ds(pl.multiple_of(col * band, band), band)]

    group = tables_ref.shape[1]
    loads[2].wait()

    def build(step, carry):
        cosine = tables_ref[0, pl.ds(step, 1)]
        sine = tables_ref[1, pl.ds(step, 1)]
        high, low = split(cosine * tables_ref[2] + sine * tables_ref[3])
        at = pl.ds(pl.multiple_of(step * group, group), group)
        c_high[at] = high
        c_low[at] = low
        return carry

    lax.fori_loop(0, total // group, build, 0)

    def filters():
        shape = (band, total)
        q = me * band + lax.broadcasted_iota(jnp.int32, shape, 0)
        p = lax.broadcasted_iota(jnp.int32, shape, 1)
        wave_number = signed_squares(p, total) + signed_squares(q, total)
        normalize = 1.0 / (total * total)
        growths, forcings = [], []
        for diffusion, decay_rate in (
            (SUBSTRATE_DIFFUSION, FEED_RATE),
            (ACTIVATOR_DIFFUSION, FEED_RATE + KILL_RATE),
        ):
            linear = -diffusion * wave_number - decay_rate
            growth = jnp.exp(linear * (0.5 * TIME_STEP))
            growths.append(growth * normalize)
            forcings.append((growth - 1.0) / linear * normalize)
        return growths, forcings

    quarter = band // 4
    per_chunk = chunk // band
    chunks = total // chunk

    def remote(leg, other):
        step = lax.rem(other - me + devices, devices)
        return pltpu.make_async_remote_copy(
            src_ref=send.at[leg, other],
            dst_ref=recv.at[leg, me],
            send_sem=s_send.at[leg, step],
            recv_sem=s_recv.at[leg, step],
            device_id=(other // cols, lax.rem(other, cols)),
            device_id_type=MESH,
        )

    def spread(field):
        high, low = split(field)
        for copy_at in range(4):
            wide[copy_at * band : (copy_at + 1) * band] = high
            wide[(4 + copy_at) * band : (5 + copy_at) * band] = low

    def launch(leg):
        lane = lax.broadcasted_iota(jnp.int32, (per_chunk, quarter, LANES), 2) // (LANES // 4)

        def body(step, carry):
            number = lax.rem(row * chunks // rows + chunks // 2 + step, chunks)
            at = pl.ds(pl.multiple_of(number * chunk, chunk), chunk)
            both = contract_last(c_high[at], wide[...])
            out = both[:, :LANES] + both[:, LANES:] + contract_last(c_low[at], wide[:LANES])
            out = out.reshape(per_chunk, band, LANES)
            first = number * per_chunk
            piece = out[:, :quarter]
            for j in range(1, 4):
                piece = jnp.where(lane == j, out[:, j * quarter : (j + 1) * quarter], piece)
            send[leg, pl.ds(first, per_chunk)] = piece

            def start(index, carry):
                other = first + index

                @pl.when(other != me)
                def _():
                    remote(leg, other).start()

                return carry

            return lax.fori_loop(0, per_chunk, start, carry)

        lax.fori_loop(0, chunks, body, 0)
        recv[leg, me] = send[leg, me]

    def land(leg):
        def wait(step, carry):
            remote(leg, lax.rem(me + step, devices)).wait_recv()
            return carry

        lax.fori_loop(1, devices, wait, 0)
        for g in range(devices // 4):
            pieces = block_transpose([recv[leg, 4 * g + k] for k in range(4)])
            at = slice(g * LANES, (g + 1) * LANES)
            for j in range(4):
                high, low = split(pieces[j])
                packed[j * quarter : (j + 1) * quarter, at] = high.astype(jnp.float32)
                packed[band + j * quarter : band + (j + 1) * quarter, at] = low.astype(
                    jnp.float32
                )
        both = packed[...].astype(jnp.bfloat16)
        out = []
        for number in range(chunks):
            at = slice(number * chunk, (number + 1) * chunk)
            dot = functools.partial(jnp.dot, preferred_element_type=jnp.float32)
            product = dot(both, c_high[:, at])
            out.append(product[:band] + product[band:] + dot(both[:band], c_low[:, at]))
        return out

    def gathered(field):
        for copy in in_copies[field]:
            copy.wait_recv()
        return jnp.concatenate([x_in[field, block] for block in range(cols)], axis=1)

    v = gathered(1)
    spread(v)
    pl.semaphore_wait(ready, rows - 1)
    launch(0)
    u = gathered(0)
    v = jnp.concatenate([x_in[1, block] for block in range(cols)], axis=1)
    spread(u * v * v)
    launch(1)
    spread(jnp.concatenate([x_in[0, block] for block in range(cols)], axis=1))
    launch(2)
    growth, forcing = filters()
    activator = growth[1] * jnp.concatenate(land(0), axis=1)
    reaction = jnp.concatenate(land(1), axis=1)
    spread(activator + forcing[1] * reaction)
    launch(3)
    reaction = forcing[0] * reaction
    spread(growth[0] * jnp.concatenate(land(2), axis=1) - reaction)
    launch(4)

    zero = -(FEED_RATE)
    constant = FEED_RATE * math.expm1(zero * 0.5 * TIME_STEP) / zero
    def out_copy(step, field):
        ref = (out_u, out_v)[field]
        other = lax.rem(col + step, cols)
        return pltpu.make_async_remote_copy(
            src_ref=result.at[field, other],
            dst_ref=ref.at[pl.ds(pl.multiple_of(col * band, band), band)],
            send_sem=out_send.at[field, step],
            recv_sem=out_recv.at[field, step],
            device_id=(row, other),
            device_id_type=MESH,
        )

    out_copies = []
    for leg, field, extra in ((3, 1, 0.0), (4, 0, constant)):
        for number, out in enumerate(land(leg)):
            result[field, number] = out + extra
        for step in range(1, cols):
            out_copies.append(out_copy(step, field))
            out_copies[-1].start()
        ref = (out_u, out_v)[field]
        ref[pl.ds(pl.multiple_of(col * band, band), band)] = result[field, col]
    for copy in in_copies[0] + in_copies[1]:
        copy.wait_send()

    def drain(step, carry):
        for leg in range(5):
            remote(leg, lax.rem(me + step, devices)).wait_send()
        return carry

    lax.fori_loop(1, devices, drain, 0)
    for copy in out_copies:
        copy.wait()


def tables(total, group):
    wave = np.arange(total)

    def angles(index):
        return 2.0 * np.pi / total * (index[:, None] * wave[None, :] % total)

    coarse = angles(np.arange(total // group) * group)
    fine = angles(np.arange(group))
    return jnp.asarray(
        np.stack(
            (
                np.cos(coarse),
                np.sin(coarse),
                np.cos(fine) + np.sin(fine),
                np.cos(fine) - np.sin(fine),
            )
        ),
        jnp.float32,
    )


def on_device_fused(rows, cols, substrate, activator):
    height, width = substrate.shape
    total = width * cols
    band = height // cols
    devices = rows * cols
    bf16, f32 = jnp.bfloat16, jnp.float32
    dma = pltpu.SemaphoreType.DMA
    block = jax.ShapeDtypeStruct(substrate.shape, f32)
    vmem = pl.BlockSpec(memory_space=pltpu.VMEM)
    return pl.pallas_call(
        functools.partial(section_kernel, rows, cols),
        out_shape=(block, block),
        in_specs=[pl.BlockSpec(memory_space=pltpu.HBM)] * 3,
        out_specs=(vmem, vmem),
        scratch_shapes=[
            pltpu.VMEM(substrate.shape, f32),
            pltpu.VMEM(substrate.shape, f32),
            pltpu.VMEM((4, 32, total), f32),
            pltpu.VMEM((total, total), bf16),
            pltpu.VMEM((total, total), bf16),
            pltpu.VMEM((2, cols, band, width), f32),
            pltpu.VMEM((2 * band, total), f32),
            pltpu.VMEM((8 * band, total), bf16),
            pltpu.VMEM((5, devices, band // 4, LANES), f32),
            pltpu.VMEM((5, devices, band // 4, LANES), f32),
            pltpu.VMEM((2, cols, band, width), f32),
            pltpu.SemaphoreType.REGULAR,
            dma((3,)),
            dma((2, cols)),
            dma((2, cols)),
            dma((5, devices)),
            dma((5, devices)),
            dma((2, cols)),
            dma((2, cols)),
        ],
        compiler_params=pltpu.CompilerParams(
            collective_id=0, has_side_effects=True, vmem_limit_bytes=48 * 2**20
        ),
    )(substrate, activator, tables(total, 32))


def dispatch(rows, cols, substrate, activator):
    height, width = substrate.shape
    total = width * cols
    band = height // cols
    dense_fits = total * total * 4 <= 16 * 2**20
    fits = height * rows == total and 4 * band == LANES and band * rows * cols == total
    if fits and dense_fits and width == 256:
        return on_device_fused(rows, cols, substrate, activator)
    return on_device(substrate, activator)


def solution(mesh):
    in_specs = (P("row", "col"), P("row", "col"))
    out_specs = (P("row", "col"), P("row", "col"))
    return jax.shard_map(
        functools.partial(dispatch, mesh.shape["row"], mesh.shape["col"]),
        mesh=mesh,
        in_specs=in_specs,
        out_specs=out_specs,
        check_vma=False,
    )
```

profile of v0, /device:TPU:0, one launch (start us, length us, event | category | flops | bytes accessed | tf_op | source)
XLA Modules:
  0.0 43.7 jit_solution(6396149049605781608)
XLA Ops:
  0.6 0.0 copy-start
  0.6 1.0 %copy-done = f32[4,32,1024]{2,1,0:T(8,128)S(1)} copy-done((f32[4,32,1024]{2,1,0:T(8,128)S(1)}, f32[4,32,1024]{2,1,0:T(8,128)}, u32[]{:S(2)}) %copy-start) | copy-done | bytes 524312
  1.7 0.0 copy-start.1
  1.7 0.9 %copy-done.1 = f32[128,256]{1,0:T(8,128)S(1)} copy-done((f32[128,256]{1,0:T(8,128)S(1)}, f32[128,256]{1,0:T(8,128)}, u32[]{:S(2)}) %copy-start.1) | copy-done | bytes 131096
  2.6 0.0 copy-start.2
  2.6 0.9 %copy-done.2 = f32[128,256]{1,0:T(8,128)S(1)} copy-done((f32[128,256]{1,0:T(8,128)S(1)}, f32[128,256]{1,0:T(8,128)}, u32[]{:S(2)}) %copy-start.2) | copy-done | bytes 131096
  3.5 38.9 %shard_map.50 = (f32[128,256]{1,0:T(8,128)S(1)}, f32[128,256]{1,0:T(8,128)S(1)}) custom-call(f32[128,256]{1,0:T(8,128)S(1)} %copy-done.1, f32[128,256]{1,0:T(8,128)S(1)} %copy-done.2, f32[4,32,1024]{2,1,0:T(8,128)S(1)} %copy-done), custom_call_target="tpu_custom_call" | custom-call | tf_op jit(solution)/shard_map/pallas_call | solution.py:427
  42.4 0.7 %copy.7 = f32[128,256]{1,0:T(8,128)} copy(f32[128,256]{1,0:T(8,128)S(1)} %get-tuple-element.4) | data formatting | bytes 262144
  43.0 0.7 %copy.8 = f32[128,256]{1,0:T(8,128)} copy(f32[128,256]{1,0:T(8,128)S(1)} %get-tuple-element.5) | data formatting | bytes 262144
Async XLA Ops:
  0.6 1.0 %copy-start = (f32[4,32,1024]{2,1,0:T(8,128)S(1)}, f32[4,32,1024]{2,1,0:T(8,128)}, u32[]{:S(2)}) copy-start(f32[4,32,1024]{2,1,0:T(8,128)} %constant.2.clone.tables_hbm) | copy-start | bytes 1572868
  1.7 0.9 %copy-start.1 = (f32[128,256]{1,0:T(8,128)S(1)}, f32[128,256]{1,0:T(8,128)}, u32[]{:S(2)}) copy-start(f32[128,256]{1,0:T(8,128)} %u_hbm.1) | copy-start | bytes 393220
  2.6 0.9 %copy-start.2 = (f32[128,256]{1,0:T(8,128)S(1)}, f32[128,256]{1,0:T(8,128)}, u32[]{:S(2)}) copy-start(f32[128,256]{1,0:T(8,128)} %v_hbm.1) | copy-start | bytes 393220
where the time goes:
time: 43.9 us; the launch traced here: 43.7 us
  Pallas kernels  38.9 us (89%)
  local copies, waits for them, and re-layouts  4.16 us (9%)
  between operations  0.65 us (1%)
    pallas_call x1, Pallas kernels, on_device_fused(): pl.pallas_call(functools.partial(section_kernel, rows, cols), out_shape=(...  38.9 us
    unnamed x8, local copies, waits for them, and re-layouts  4.16 us

commit v1 on v0

--- a/solution.py
+++ b/solution.py
@@ -173,7 +173,7 @@
 
 
 def section_kernel(
-    rows, cols, u_hbm, v_hbm, tables_hbm, out_u, out_v, u_ref, v_ref, tables_ref,
+    rows, cols, u_hbm, v_hbm, tables_hbm, sections, u_ref, v_ref, tables_ref,
     c_high, c_low, x_in, packed, wide, send, recv, result,
     ready, load_sem, in_send, in_recv, s_send, s_recv, out_send, out_recv,
 ):
@@ -248,7 +248,6 @@
         q = me * band + lax.broadcasted_iota(jnp.int32, shape, 0)
         p = lax.broadcasted_iota(jnp.int32, shape, 1)
         wave_number = signed_squares(p, total) + signed_squares(q, total)
-        normalize = 1.0 / (total * total)
         growths, forcings = [], []
         for diffusion, decay_rate in (
             (SUBSTRATE_DIFFUSION, FEED_RATE),
@@ -256,8 +255,8 @@
         ):
             linear = -diffusion * wave_number - decay_rate
             growth = jnp.exp(linear * (0.5 * TIME_STEP))
-            growths.append(growth * normalize)
-            forcings.append((growth - 1.0) / linear * normalize)
+            growths.append(growth)
+            forcings.append((growth - 1.0) / linear)
         return growths, forcings
 
     quarter = band // 4
@@ -358,10 +357,8 @@
     spread(growth[0] * jnp.concatenate(land(2), axis=1) - reaction)
     launch(4)
 
-    zero = -(FEED_RATE)
-    constant = FEED_RATE * math.expm1(zero * 0.5 * TIME_STEP) / zero
     def out_copy(step, field):
-        ref = (out_u, out_v)[field]
+        ref = sections.at[field]
         other = lax.rem(col + step, cols)
         return pltpu.make_async_remote_copy(
             src_ref=result.at[field, other],
@@ -373,14 +370,13 @@
         )
 
     out_copies = []
-    for leg, field, extra in ((3, 1, 0.0), (4, 0, constant)):
+    for leg, field in ((3, 1), (4, 0)):
         for number, out in enumerate(land(leg)):
-            result[field, number] = out + extra
+            result[field, number] = out
         for step in range(1, cols):
             out_copies.append(out_copy(step, field))
             out_copies[-1].start()
-        ref = (out_u, out_v)[field]
-        ref[pl.ds(pl.multiple_of(col * band, band), band)] = result[field, col]
+        sections[field, pl.ds(pl.multiple_of(col * band, band), band)] = result[field, col]
     for copy in in_copies[0] + in_copies[1]:
         copy.wait_send()
 
@@ -422,13 +418,13 @@
     devices = rows * cols
     bf16, f32 = jnp.bfloat16, jnp.float32
     dma = pltpu.SemaphoreType.DMA
-    block = jax.ShapeDtypeStruct(substrate.shape, f32)
     vmem = pl.BlockSpec(memory_space=pltpu.VMEM)
-    return pl.pallas_call(
+    operands = (substrate, activator, tables(total, 32))
+    sections = pl.pallas_call(
         functools.partial(section_kernel, rows, cols),
-        out_shape=(block, block),
+        out_shape=jax.ShapeDtypeStruct((2,) + substrate.shape, f32),
         in_specs=[pl.BlockSpec(memory_space=pltpu.HBM)] * 3,
-        out_specs=(vmem, vmem),
+        out_specs=vmem,
         scratch_shapes=[
             pltpu.VMEM(substrate.shape, f32),
             pltpu.VMEM(substrate.shape, f32),
@@ -453,7 +449,11 @@
         compiler_params=pltpu.CompilerParams(
             collective_id=0, has_side_effects=True, vmem_limit_bytes=48 * 2**20
         ),
-    )(substrate, activator, tables(total, 32))
+    )(*(pltpu.with_memory_space_constraint(value, pltpu.HBM) for value in operands))
+    zero = -(FEED_RATE)
+    constant = FEED_RATE * math.expm1(zero * 0.5 * TIME_STEP) / zero
+    normalize = 1.0 / (total * total)
+    return sections[0] * normalize + constant, sections[1] * normalize
 
 
 def dispatch(rows, cols, substrate, activator):

time: 43.9 us -> 40.1 us (0.913)
  local copies, waits for them, and re-layouts: 4.16 us -> 0 us
  other arithmetic: 0 us -> 0.72 us
    unnamed x8 -> x0, local copies, waits for them, and re-layouts: 4.16 us -> none
    mul x0 -> x1, other arithmetic: none -> 0.72 us  [on_device_fused(): return (sections[0] * normalize + constant, sections[1] * normalize)]
where the time goes in v1:
time: 40.1 us; the launch traced here: 39.9 us
  Pallas kernels  38.6 us (96%)
  other arithmetic  0.72 us (2%)
  between operations  0.64 us (2%)
    pallas_call x1, Pallas kernels, on_device_fused(): pl.pallas_call(functools.partial(section_kernel, rows, cols), out_shape=j...  38.6 us

profile of v1, /device:TPU:0, one launch (start us, length us, event | category | flops | bytes accessed | tf_op | source)
XLA Modules:
  0.0 39.9 jit_solution(11611868166550384147)
XLA Ops:
  0.6 38.6 %shard_map.50 = f32[2,128,256]{2,1,0:T(8,128)S(1)} custom-call(f32[128,256]{1,0:T(8,128)} %u_hbm.1, f32[128,256]{1,0:T(8,128)} %v_hbm.1, f32[4,32,1024]{2,1,0:T(8,128)} %constant.6.clone.tables_hbm), custom_call_target="tpu_custom_call" | custom-call | tf_op jit(solution)/shard_map/pallas_call | solution.py:423
  39.2 0.7 %multiply_bitcast_fusion = (f32[128,256]{1,0:T(8,128)}, f32[128,256]{1,0:T(8,128)}) fusion(f32[2,128,256]{2,1,0:T(8,128)S(1)} %shard_map.50), kind=kLoop, calls=%fused_computation | loop fusion | flops 98304 | bytes 524288 | tf_op jit(solution)/shard_map/mul | solution.py:456

commit v2 on v1

--- a/solution.py
+++ b/solution.py
@@ -174,14 +174,16 @@
 
 def section_kernel(
     rows, cols, u_hbm, v_hbm, tables_hbm, sections, u_ref, v_ref, tables_ref,
-    c_high, c_low, x_in, packed, wide, send, recv, result,
+    forth, flipped, x_in, packed, wide, filters, spectrum, send, recv, result,
     ready, load_sem, in_send, in_recv, s_send, s_recv, out_send, out_recv,
 ):
     devices = rows * cols
     total = u_ref.shape[1] * cols
+    half = total // 2
     band = u_ref.shape[0] // cols
-    width = u_ref.shape[1]
-    chunk = 256
+    quarter = band // 4
+    chunk = half // 2
+    group = 32
     row = lax.axis_index("row")
     col = lax.axis_index("col")
     me = row * cols + col
@@ -189,7 +191,7 @@
     loads = [
         pltpu.make_async_copy(source, target, load_sem.at[index])
         for index, (source, target) in enumerate(
-            ((u_hbm, u_ref), (v_hbm, v_ref), (tables_hbm, tables_ref))
+            ((v_hbm, v_ref), (u_hbm, u_ref), (tables_hbm, tables_ref))
         )
     ]
     for load in loads:
@@ -228,141 +230,196 @@
         greet(ready, lax.rem(row + step, rows), col)
     for field, ref in enumerate((u_ref, v_ref)):
         x_in[field, col] = ref[pl.ds(pl.multiple_of(col * band, band), band)]
-
-    group = tables_ref.shape[1]
     loads[2].wait()
 
-    def build(step, carry):
-        cosine = tables_ref[0, pl.ds(step, 1)]
-        sine = tables_ref[1, pl.ds(step, 1)]
-        high, low = split(cosine * tables_ref[2] + sine * tables_ref[3])
-        at = pl.ds(pl.multiple_of(step * group, group), group)
-        c_high[at] = high
-        c_low[at] = low
-        return carry
-
-    lax.fori_loop(0, total // group, build, 0)
-
-    def filters():
+    def build(target, coarse, fine):
+        def body(step, carry):
+            cosine = tables_ref[6 + coarse, pl.ds(step, 1)]
+            sine = tables_ref[7 + coarse, pl.ds(step, 1)]
+            high, low = split(cosine * tables_ref[fine] + sine * tables_ref[fine + 1])
+            at = pl.ds(pl.multiple_of(step * group, group), group)
+            target[0, at] = high
+            target[1, at] = low
+            return carry
+
+        lax.fori_loop(0, half // group, body, 0)
+
+    build(forth.at[0], 0, 0)
+    build(forth.at[1], 0, 2)
+
+    def wave(position):
+        return jnp.where(position < half, 2 * position, 2 * (position - half) + 1)
+
+    def fill_filters():
         shape = (band, total)
-        q = me * band + lax.broadcasted_iota(jnp.int32, shape, 0)
-        p = lax.broadcasted_iota(jnp.int32, shape, 1)
+        q = wave(me * band + lax.broadcasted_iota(jnp.int32, shape, 0))
+        p = wave(lax.broadcasted_iota(jnp.int32, shape, 1))
         wave_number = signed_squares(p, total) + signed_squares(q, total)
-        growths, forcings = [], []
-        for diffusion, decay_rate in (
+        for index, (diffusion, decay_rate) in enumerate((
             (SUBSTRATE_DIFFUSION, FEED_RATE),
             (ACTIVATOR_DIFFUSION, FEED_RATE + KILL_RATE),
-        ):
+        )):
             linear = -diffusion * wave_number - decay_rate
             growth = jnp.exp(linear * (0.5 * TIME_STEP))
-            growths.append(growth)
-            forcings.append((growth - 1.0) / linear)
-        return growths, forcings
-
-    quarter = band // 4
-    per_chunk = chunk // band
-    chunks = total // chunk
+            filters[2 * index] = growth
+            filters[2 * index + 1] = (growth - 1.0) / linear
 
     def remote(leg, other):
-        step = lax.rem(other - me + devices, devices)
         return pltpu.make_async_remote_copy(
             src_ref=send.at[leg, other],
             dst_ref=recv.at[leg, me],
-            send_sem=s_send.at[leg, step],
-            recv_sem=s_recv.at[leg, step],
+            send_sem=s_send.at[leg],
+            recv_sem=s_recv.at[leg],
             device_id=(other // cols, lax.rem(other, cols)),
             device_id_type=MESH,
         )
 
-    def spread(field):
+    def all_of(leg):
+        others = pl.ds(0, devices - 1)
+        other = lax.rem(me + 1, devices)
+        return pltpu.make_async_remote_copy(
+            src_ref=send.at[leg, others],
+            dst_ref=recv.at[leg, others],
+            send_sem=s_send.at[leg],
+            recv_sem=s_recv.at[leg],
+            device_id=(other // cols, lax.rem(other, cols)),
+            device_id_type=MESH,
+        )
+
+    def spread(parity, field):
         high, low = split(field)
         for copy_at in range(4):
-            wide[copy_at * band : (copy_at + 1) * band] = high
-            wide[(4 + copy_at) * band : (5 + copy_at) * band] = low
-
-    def launch(leg):
-        lane = lax.broadcasted_iota(jnp.int32, (per_chunk, quarter, LANES), 2) // (LANES // 4)
-
-        def body(step, carry):
-            number = lax.rem(row * chunks // rows + chunks // 2 + step, chunks)
-            at = pl.ds(pl.multiple_of(number * chunk, chunk), chunk)
-            both = contract_last(c_high[at], wide[...])
-            out = both[:, :LANES] + both[:, LANES:] + contract_last(c_low[at], wide[:LANES])
-            out = out.reshape(per_chunk, band, LANES)
-            first = number * per_chunk
-            piece = out[:, :quarter]
-            for j in range(1, 4):
-                piece = jnp.where(lane == j, out[:, j * quarter : (j + 1) * quarter], piece)
-            send[leg, pl.ds(first, per_chunk)] = piece
-
-            def start(index, carry):
-                other = first + index
-
-                @pl.when(other != me)
-                def _():
-                    remote(leg, other).start()
-
-                return carry
-
-            return lax.fori_loop(0, per_chunk, start, carry)
-
-        lax.fori_loop(0, chunks, body, 0)
+            wide[parity, copy_at * band : (copy_at + 1) * band] = high
+            wide[parity, (4 + copy_at) * band : (5 + copy_at) * band] = low
+
+    def product(high, low, parity):
+        both = contract_last(high, wide[parity])
+        return both[:, :LANES] + both[:, LANES:] + contract_last(low, wide[parity, :LANES])
+
+    def stage(leg, first, values):
+        count = values.shape[0] // band
+        lane = lax.broadcasted_iota(jnp.int32, (count, quarter, LANES), 2) // (LANES // 4)
+        out = values.reshape(count, band, LANES)
+        piece = out[:, :quarter]
+        for j in range(1, 4):
+            piece = jnp.where(lane == j, out[:, j * quarter : (j + 1) * quarter], piece)
+        send[leg, pl.ds(first, count)] = piece
+
+
+    def begin(leg, other):
+        remote(leg, other).start()
+
+    def forward(leg):
+        count = devices // 2
+        mine = me // count
+        for step in range(2):
+            parity = lax.rem(mine + 1 + step, 2)
+            stage(leg, parity * count, product(forth[parity, 0], forth[parity, 1], parity))
+            for k in range(step, count):
+                begin(leg, parity * count + lax.rem(me + k, count))
         recv[leg, me] = send[leg, me]
 
-    def land(leg):
-        def wait(step, carry):
-            remote(leg, lax.rem(me + step, devices)).wait_recv()
-            return carry
-
-        lax.fori_loop(1, devices, wait, 0)
-        for g in range(devices // 4):
-            pieces = block_transpose([recv[leg, 4 * g + k] for k in range(4)])
-            at = slice(g * LANES, (g + 1) * LANES)
-            for j in range(4):
-                high, low = split(pieces[j])
-                packed[j * quarter : (j + 1) * quarter, at] = high.astype(jnp.float32)
-                packed[band + j * quarter : band + (j + 1) * quarter, at] = low.astype(
-                    jnp.float32
-                )
-        both = packed[...].astype(jnp.bfloat16)
-        out = []
-        for number in range(chunks):
-            at = slice(number * chunk, (number + 1) * chunk)
-            dot = functools.partial(jnp.dot, preferred_element_type=jnp.float32)
-            product = dot(both, c_high[:, at])
-            out.append(product[:band] + product[band:] + dot(both[:band], c_low[:, at]))
-        return out
-
-    def gathered(field):
-        for copy in in_copies[field]:
-            copy.wait_recv()
-        return jnp.concatenate([x_in[field, block] for block in range(cols)], axis=1)
-
-    v = gathered(1)
-    spread(v)
+    def inverse(leg):
+        count = devices // 4
+        side = me // (2 * count)
+        mine = lax.rem(me, 2 * count) // count
+        for step in range(2):
+            part = lax.rem(mine + 1 + step, 2)
+            at = pl.ds(pl.multiple_of(part * chunk, chunk), chunk)
+            first = product(forth[0, 0, at], forth[0, 1, at], 0)
+            second = product(flipped[0, at], flipped[1, at], 1)
+            stage(leg, part * count, first + second)
+            stage(leg, part * count + 2 * count, first - second)
+            for k in range(count):
+                other = part * count + lax.rem(me + k, count)
+                begin(leg, other + 2 * count * (1 - side))
+                if step == 0 or k > 0:
+                    begin(leg, other + 2 * count * side)
+        recv[leg, me] = send[leg, me]
+
+    def pack(parity, rows_at, pair):
+        high, low = split(jnp.concatenate(pair, axis=0))
+        at = slice(rows_at[1] * LANES, (rows_at[1] + 1) * LANES)
+        first = rows_at[0] * 2 * quarter
+        packed[parity, first : first + 2 * quarter, at] = high
+        packed[parity, band + first : band + first + 2 * quarter, at] = low
+
+    def turned(leg, g):
+        return block_transpose([recv[leg, 4 * g + k] for k in range(4)])
+
+    def dots(parity, high, low):
+        dot = functools.partial(jnp.dot, preferred_element_type=jnp.float32)
+        both = packed[parity]
+        out = dot(both, high)
+        return out[:band] + out[band:] + dot(both[:band], low)
+
+    def land_forward(leg):
+        all_of(leg).wait_recv()
+        groups = devices // 8
+        for g in range(groups):
+            first, second = turned(leg, g), turned(leg, g + groups)
+            for pair in range(2):
+                a = [first[2 * pair], first[2 * pair + 1]]
+                b = [second[2 * pair], second[2 * pair + 1]]
+                pack(0, (pair, g), [m + n for m, n in zip(a, b)])
+                pack(1, (pair, g), [m - n for m, n in zip(a, b)])
+        return jnp.concatenate(
+            [dots(0, forth[0, 0], forth[0, 1]), dots(1, flipped[0], flipped[1])], axis=1
+        )
+
+    def land_inverse(leg):
+        all_of(leg).wait_recv()
+        groups = devices // 8
+        for parity in range(2):
+            for g in range(groups):
+                pieces = turned(leg, parity * groups + g)
+                for pair in range(2):
+                    pack(parity, (pair, g), [pieces[2 * pair], pieces[2 * pair + 1]])
+        first = dots(0, forth[0, 0], forth[0, 1])
+        second = dots(1, forth[1, 0], forth[1, 1])
+        return first + second, first - second
+
+    def gathered(field, start):
+        return jnp.concatenate([x_in[field, start + block] for block in range(cols // 2)], axis=1)
+
+    def spread_field(lower, upper):
+        spread(0, lower + upper)
+        spread(1, lower - upper)
+
+    def halves(field):
+        return gathered(field, 0), gathered(field, cols // 2)
+
+    for copy in in_copies[1]:
+        copy.wait_recv()
+    spread_field(*halves(1))
     pl.semaphore_wait(ready, rows - 1)
-    launch(0)
-    u = gathered(0)
-    v = jnp.concatenate([x_in[1, block] for block in range(cols)], axis=1)
-    spread(u * v * v)
-    launch(1)
-    spread(jnp.concatenate([x_in[0, block] for block in range(cols)], axis=1))
-    launch(2)
-    growth, forcing = filters()
-    activator = growth[1] * jnp.concatenate(land(0), axis=1)
-    reaction = jnp.concatenate(land(1), axis=1)
-    spread(activator + forcing[1] * reaction)
-    launch(3)
-    reaction = forcing[0] * reaction
-    spread(growth[0] * jnp.concatenate(land(2), axis=1) - reaction)
-    launch(4)
+    forward(0)
+    for copy in in_copies[0]:
+        copy.wait_recv()
+    spread_field(*(u * v * v for u, v in zip(halves(0), halves(1))))
+    forward(1)
+    spread_field(*halves(0))
+    forward(2)
+    build(flipped, 2, 4)
+    fill_filters()
+
+    def spread_spectrum(values):
+        spread(0, values[:, :half])
+        spread(1, values[:, half:])
+
+    activator = filters[2] * land_forward(0)
+    reaction = land_forward(1)
+    spread_spectrum(activator + filters[3] * reaction)
+    spectrum[...] = filters[1] * reaction
+    inverse(3)
+    spread_spectrum(filters[0] * land_forward(2) - spectrum[...])
+    inverse(4)
 
     def out_copy(step, field):
-        ref = sections.at[field]
         other = lax.rem(col + step, cols)
         return pltpu.make_async_remote_copy(
             src_ref=result.at[field, other],
-            dst_ref=ref.at[pl.ds(pl.multiple_of(col * band, band), band)],
+            dst_ref=sections.at[field, pl.ds(pl.multiple_of(col * band, band), band)],
             send_sem=out_send.at[field, step],
             recv_sem=out_recv.at[field, step],
             device_id=(row, other),
@@ -371,44 +428,39 @@
 
     out_copies = []
     for leg, field in ((3, 1), (4, 0)):
-        for number, out in enumerate(land(leg)):
-            result[field, number] = out
+        for side, out in enumerate(land_inverse(leg)):
+            for block in range(cols // 2):
+                at = slice(block * half * 2 // cols, (block + 1) * half * 2 // cols)
+                result[field, side * (cols // 2) + block] = out[:, at]
         for step in range(1, cols):
             out_copies.append(out_copy(step, field))
             out_copies[-1].start()
         sections[field, pl.ds(pl.multiple_of(col * band, band), band)] = result[field, col]
     for copy in in_copies[0] + in_copies[1]:
         copy.wait_send()
-
-    def drain(step, carry):
-        for leg in range(5):
-            remote(leg, lax.rem(me + step, devices)).wait_send()
-        return carry
-
-    lax.fori_loop(1, devices, drain, 0)
+    for leg in range(5):
+        all_of(leg).wait_send()
     for copy in out_copies:
         copy.wait()
 
 
 def tables(total, group):
-    wave = np.arange(total)
-
-    def angles(index):
-        return 2.0 * np.pi / total * (index[:, None] * wave[None, :] % total)
-
-    coarse = angles(np.arange(total // group) * group)
-    fine = angles(np.arange(group))
-    return jnp.asarray(
-        np.stack(
-            (
-                np.cos(coarse),
-                np.sin(coarse),
-                np.cos(fine) + np.sin(fine),
-                np.cos(fine) - np.sin(fine),
-            )
-        ),
-        jnp.float32,
-    )
+    half = total // 2
+    short, wave = np.arange(group), np.arange(half)
+    coarse = np.arange(half // group) * group
+
+    def angles(left, right):
+        return 2.0 * np.pi / total * (left[:, None] * right[None, :] % total)
+
+    parts = []
+    for fine in (
+        angles(2 * short, wave), angles(2 * short + 1, wave), angles(short, 2 * wave + 1)
+    ):
+        parts += [np.cos(fine) + np.sin(fine), np.cos(fine) - np.sin(fine)]
+    for rough in (angles(2 * coarse, wave), angles(coarse, 2 * wave + 1)):
+        parts += [np.cos(rough), np.sin(rough)]
+    parts = [np.pad(part, ((0, group - part.shape[0]), (0, 0))) for part in parts]
+    return jnp.asarray(np.stack(parts), jnp.float32)
 
 
 def on_device_fused(rows, cols, substrate, activator):
@@ -416,6 +468,7 @@
     total = width * cols
     band = height // cols
     devices = rows * cols
+    half = total // 2
     bf16, f32 = jnp.bfloat16, jnp.float32
     dma = pltpu.SemaphoreType.DMA
     vmem = pl.BlockSpec(memory_space=pltpu.VMEM)
@@ -428,12 +481,14 @@
         scratch_shapes=[
             pltpu.VMEM(substrate.shape, f32),
             pltpu.VMEM(substrate.shape, f32),
-            pltpu.VMEM((4, 32, total), f32),
-            pltpu.VMEM((total, total), bf16),
-            pltpu.VMEM((total, total), bf16),
+            pltpu.VMEM((10, 32, half), f32),
+            pltpu.VMEM((2, 2, half, half), bf16),
+            pltpu.VMEM((2, half, half), bf16),
             pltpu.VMEM((2, cols, band, width), f32),
-            pltpu.VMEM((2 * band, total), f32),
-            pltpu.VMEM((8 * band, total), bf16),
+            pltpu.VMEM((2, 2 * band, half), bf16),
+            pltpu.VMEM((2, 8 * band, half), bf16),
+            pltpu.VMEM((4, band, total), f32),
+            pltpu.VMEM((band, total), f32),
             pltpu.VMEM((5, devices, band // 4, LANES), f32),
             pltpu.VMEM((5, devices, band // 4, LANES), f32),
             pltpu.VMEM((2, cols, band, width), f32),
@@ -441,8 +496,8 @@
             dma((3,)),
             dma((2, cols)),
             dma((2, cols)),
-            dma((5, devices)),
-            dma((5, devices)),
+            dma((5,)),
+            dma((5,)),
             dma((2, cols)),
             dma((2, cols)),
         ],

time: 40.1 us -> 35.2 us (0.88)
  Pallas kernels: 38.6 us -> 33.7 us
    pallas_call x1, Pallas kernels: 38.6 us -> 33.7 us  [on_device_fused(): pl.pallas_call(functools.partial(section_kernel, rows, cols), out_shape=j...]
where the time goes in v2:
time: 35.2 us; the launch traced here: 35.1 us
  Pallas kernels  33.7 us (96%)
  other arithmetic  0.72 us (2%)
  between operations  0.64 us (2%)
    pallas_call x1, Pallas kernels, on_device_fused(): pl.pallas_call(functools.partial(section_kernel, rows, cols), out_shape=j...  33.7 us
    mul x1, other arithmetic, on_device_fused(): return (sections[0] * normalize + constant, sections[1] * normalize)  0.72 us

profile of v2, /device:TPU:0, one launch (start us, length us, event | category | flops | bytes accessed | tf_op | source)
XLA Modules:
  0.0 35.1 jit_solution(11293216405073334140)
XLA Ops:
  0.6 33.7 %shard_map.50 = f32[2,128,256]{2,1,0:T(8,128)S(1)} custom-call(f32[128,256]{1,0:T(8,128)} %u_hbm.1, f32[128,256]{1,0:T(8,128)} %v_hbm.1, f32[10,32,512]{2,1,0:T(8,128)} %constant.6.clone.tables_hbm), custom_call_target="tpu_custom_call" | custom-call | tf_op jit(solution)/shard_map/pallas_call | solution.py:476
  34.4 0.7 %multiply_bitcast_fusion = (f32[128,256]{1,0:T(8,128)}, f32[128,256]{1,0:T(8,128)}) fusion(f32[2,128,256]{2,1,0:T(8,128)S(1)} %shard_map.50), kind=kLoop, calls=%fused_computation | loop fusion | flops 98304 | bytes 524288 | tf_op jit(solution)/shard_map/mul | solution.py:511

commit v3 on v2

--- a/solution.py
+++ b/solution.py
@@ -217,15 +217,15 @@
         return pltpu.make_async_remote_copy(
             src_ref=ref.at[pl.ds(pl.multiple_of(other * band, band), band)],
             dst_ref=x_in.at[field, col],
-            send_sem=in_send.at[field, step],
-            recv_sem=in_recv.at[field, step],
+            send_sem=in_send.at[0],
+            recv_sem=in_recv.at[field],
             device_id=(row, other),
             device_id_type=MESH,
         )
 
-    in_copies = [[in_copy(step, field) for step in range(1, cols)] for field in range(2)]
-    for copy in in_copies[1] + in_copies[0]:
-        copy.start()
+    for field in (1, 0):
+        for step in range(1, cols):
+            in_copy(step, field).start()
     for step in range(1, rows):
         greet(ready, lax.rem(row + step, rows), col)
     for field, ref in enumerate((u_ref, v_ref)):
@@ -268,23 +268,29 @@
         return pltpu.make_async_remote_copy(
             src_ref=send.at[leg, other],
             dst_ref=recv.at[leg, me],
-            send_sem=s_send.at[leg],
+            send_sem=s_send.at[0],
             recv_sem=s_recv.at[leg],
             device_id=(other // cols, lax.rem(other, cols)),
             device_id_type=MESH,
         )
 
-    def all_of(leg):
-        others = pl.ds(0, devices - 1)
-        other = lax.rem(me + 1, devices)
+    def all_of(source, target, send_sem, recv_sem):
         return pltpu.make_async_remote_copy(
-            src_ref=send.at[leg, others],
-            dst_ref=recv.at[leg, others],
-            send_sem=s_send.at[leg],
-            recv_sem=s_recv.at[leg],
-            device_id=(other // cols, lax.rem(other, cols)),
+            src_ref=source,
+            dst_ref=target,
+            send_sem=send_sem,
+            recv_sem=recv_sem,
+            device_id=(row, lax.rem(col + 1, cols)),
             device_id_type=MESH,
         )
+
+    def arrived(leg):
+        blocks = recv.at[leg, pl.ds(0, devices - 1)]
+        all_of(blocks, blocks, s_send.at[0], s_recv.at[leg]).wait_recv()
+
+    def gather(field):
+        blocks = x_in.at[field, pl.ds(0, cols - 1)]
+        all_of(blocks, blocks, in_send.at[0], in_recv.at[field]).wait_recv()
 
     def spread(parity, field):
         high, low = split(field)
@@ -306,36 +312,32 @@
         send[leg, pl.ds(first, count)] = piece
 
 
-    def begin(leg, other):
-        remote(leg, other).start()
+    def begin(leg):
+        for step in range(1, devices):
+            over = step - 1 if step < cols else step
+            turn = (3, 1, 2, 0)[over % cols]
+            other_row = lax.rem(row + over // cols, rows)
+            remote(leg, other_row * cols + lax.rem(col + turn, cols)).start()
+        recv[leg, me] = send[leg, me]
 
     def forward(leg):
-        count = devices // 2
-        mine = me // count
-        for step in range(2):
-            parity = lax.rem(mine + 1 + step, 2)
-            stage(leg, parity * count, product(forth[parity, 0], forth[parity, 1], parity))
-            for k in range(step, count):
-                begin(leg, parity * count + lax.rem(me + k, count))
-        recv[leg, me] = send[leg, me]
+        for parity in range(2):
+            stage(
+                leg,
+                parity * (devices // 2),
+                product(forth[parity, 0], forth[parity, 1], parity),
+            )
+        begin(leg)
 
     def inverse(leg):
         count = devices // 4
-        side = me // (2 * count)
-        mine = lax.rem(me, 2 * count) // count
-        for step in range(2):
-            part = lax.rem(mine + 1 + step, 2)
-            at = pl.ds(pl.multiple_of(part * chunk, chunk), chunk)
+        for part in range(2):
+            at = slice(part * chunk, (part + 1) * chunk)
             first = product(forth[0, 0, at], forth[0, 1, at], 0)
             second = product(flipped[0, at], flipped[1, at], 1)
             stage(leg, part * count, first + second)
             stage(leg, part * count + 2 * count, first - second)
-            for k in range(count):
-                other = part * count + lax.rem(me + k, count)
-                begin(leg, other + 2 * count * (1 - side))
-                if step == 0 or k > 0:
-                    begin(leg, other + 2 * count * side)
-        recv[leg, me] = send[leg, me]
+        begin(leg)
 
     def pack(parity, rows_at, pair):
         high, low = split(jnp.concatenate(pair, axis=0))
@@ -354,7 +356,7 @@
         return out[:band] + out[band:] + dot(both[:band], low)
 
     def land_forward(leg):
-        all_of(leg).wait_recv()
+        arrived(leg)
         groups = devices // 8
         for g in range(groups):
             first, second = turned(leg, g), turned(leg, g + groups)
@@ -368,7 +370,7 @@
         )
 
     def land_inverse(leg):
-        all_of(leg).wait_recv()
+        arrived(leg)
         groups = devices // 8
         for parity in range(2):
             for g in range(groups):
@@ -389,13 +391,11 @@
     def halves(field):
         return gathered(field, 0), gathered(field, cols // 2)
 
-    for copy in in_copies[1]:
-        copy.wait_recv()
+    gather(1)
     spread_field(*halves(1))
     pl.semaphore_wait(ready, rows - 1)
     forward(0)
-    for copy in in_copies[0]:
-        copy.wait_recv()
+    gather(0)
     spread_field(*(u * v * v for u, v in zip(halves(0), halves(1))))
     forward(1)
     spread_field(*halves(0))
@@ -420,28 +420,26 @@
         return pltpu.make_async_remote_copy(
             src_ref=result.at[field, other],
             dst_ref=sections.at[field, pl.ds(pl.multiple_of(col * band, band), band)],
-            send_sem=out_send.at[field, step],
-            recv_sem=out_recv.at[field, step],
+            send_sem=out_send.at[0],
+            recv_sem=out_recv.at[0],
             device_id=(row, other),
             device_id_type=MESH,
         )
 
-    out_copies = []
     for leg, field in ((3, 1), (4, 0)):
         for side, out in enumerate(land_inverse(leg)):
             for block in range(cols // 2):
                 at = slice(block * half * 2 // cols, (block + 1) * half * 2 // cols)
                 result[field, side * (cols // 2) + block] = out[:, at]
         for step in range(1, cols):
-            out_copies.append(out_copy(step, field))
-            out_copies[-1].start()
+            out_copy(step, field).start()
         sections[field, pl.ds(pl.multiple_of(col * band, band), band)] = result[field, col]
-    for copy in in_copies[0] + in_copies[1]:
-        copy.wait_send()
-    for leg in range(5):
-        all_of(leg).wait_send()
-    for copy in out_copies:
-        copy.wait()
+    sent = send.at[:, pl.ds(0, devices - 1)]
+    all_of(sent, sent, s_send.at[0], s_recv.at[0]).wait_send()
+    sent = x_in.at[:, pl.ds(0, cols - 1)]
+    all_of(sent, sent, in_send.at[0], in_recv.at[0]).wait_send()
+    sent = result.at[:, pl.ds(0, cols - 1)]
+    all_of(sent, sent, out_send.at[0], out_recv.at[0]).wait()
 
 
 def tables(total, group):
@@ -494,12 +492,12 @@
             pltpu.VMEM((2, cols, band, width), f32),
             pltpu.SemaphoreType.REGULAR,
             dma((3,)),
-            dma((2, cols)),
-            dma((2, cols)),
+            dma((1,)),
+            dma((2,)),
+            dma((1,)),
             dma((5,)),
-            dma((5,)),
-            dma((2, cols)),
-            dma((2, cols)),
+            dma((1,)),
+            dma((1,)),
         ],
         compiler_params=pltpu.CompilerParams(
             collective_id=0, has_side_effects=True, vmem_limit_bytes=48 * 2**20

time: 35.2 us -> 33.9 us (0.963)
  Pallas kernels: 33.7 us -> 32.4 us
    pallas_call x1, Pallas kernels: 33.7 us -> 32.4 us  [on_device_fused(): pl.pallas_call(functools.partial(section_kernel, rows, cols), out_shape=j...]
where the time goes in v3:
time: 33.9 us; the launch traced here: 33.8 us
  Pallas kernels  32.4 us (96%)
  other arithmetic  0.72 us (2%)
  between operations  0.64 us (2%)
    pallas_call x1, Pallas kernels, on_device_fused(): pl.pallas_call(functools.partial(section_kernel, rows, cols), out_shape=j...  32.4 us
    mul x1, other arithmetic, on_device_fused(): return (sections[0] * normalize + constant, sections[1] * normalize)  0.72 us

profile of v3, /device:TPU:0, one launch (start us, length us, event | category | flops | bytes accessed | tf_op | source)
XLA Modules:
  0.0 33.8 jit_solution(4323876685539647547)
XLA Ops:
  0.6 32.4 %shard_map.50 = f32[2,128,256]{2,1,0:T(8,128)S(1)} custom-call(f32[128,256]{1,0:T(8,128)} %u_hbm.1, f32[128,256]{1,0:T(8,128)} %v_hbm.1, f32[10,32,512]{2,1,0:T(8,128)} %constant.6.clone.tables_hbm), custom_call_target="tpu_custom_call" | custom-call | tf_op jit(solution)/shard_map/pallas_call | solution.py:474
  33.1 0.7 %multiply_bitcast_fusion = (f32[128,256]{1,0:T(8,128)}, f32[128,256]{1,0:T(8,128)}) fusion(f32[2,128,256]{2,1,0:T(8,128)S(1)} %shard_map.50), kind=kLoop, calls=%fused_computation | loop fusion | flops 98304 | bytes 524288 | tf_op jit(solution)/shard_map/mul | solution.py:509

commit v4 on v3

--- a/solution.py
+++ b/solution.py
@@ -207,8 +207,6 @@
         greet(barrier, row, lax.rem(col + step, cols))
     for step in range(1, rows):
         greet(barrier, lax.rem(row + step, rows), col)
-    for load in loads[:2]:
-        load.wait()
     pl.semaphore_wait(barrier, rows + cols - 2)
 
     def in_copy(step, field):
@@ -224,6 +222,7 @@
         )
 
     for field in (1, 0):
+        loads[1 - field].wait()
         for step in range(1, cols):
             in_copy(step, field).start()
     for step in range(1, rows):
@@ -320,6 +319,15 @@
             remote(leg, other_row * cols + lax.rem(col + turn, cols)).start()
         recv[leg, me] = send[leg, me]
 
+    def lead(leg):
+        count = devices // 2
+        for step in range(2):
+            parity = lax.rem(me // count + 1 + step, 2)
+            stage(leg, parity * count, product(forth[parity, 0], forth[parity, 1], parity))
+            for k in range(step, count):
+                remote(leg, parity * count + lax.rem(me + k, count)).start()
+        recv[leg, me] = send[leg, me]
+
     def forward(leg):
         for parity in range(2):
             stage(
@@ -328,6 +336,23 @@
                 product(forth[parity, 0], forth[parity, 1], parity),
             )
         begin(leg)
+
+    def swift(leg):
+        count = devices // 4
+        side = me // (2 * count)
+        mine = lax.rem(me, 2 * count) // count
+        for step in range(2):
+            part = lax.rem(mine + 1 + step, 2)
+            at = pl.ds(pl.multiple_of(part * chunk, chunk), chunk)
+            first = product(forth[0, 0, at], forth[0, 1, at], 0)
+            second = product(flipped[0, at], flipped[1, at], 1)
+            stage(leg, part * count, first + second)
+            stage(leg, part * count + 2 * count, first - second)
+            for away, nearest in ((1 - side, 0), (side, step)):
+                for k in range(nearest, count):
+                    other = part * count + lax.rem(me + k, count)
+                    remote(leg, other + 2 * count * away).start()
+        recv[leg, me] = send[leg, me]
 
     def inverse(leg):
         count = devices // 4
@@ -394,7 +419,7 @@
     gather(1)
     spread_field(*halves(1))
     pl.semaphore_wait(ready, rows - 1)
-    forward(0)
+    lead(0)
     gather(0)
     spread_field(*(u * v * v for u, v in zip(halves(0), halves(1))))
     forward(1)
@@ -411,7 +436,7 @@
     reaction = land_forward(1)
     spread_spectrum(activator + filters[3] * reaction)
     spectrum[...] = filters[1] * reaction
-    inverse(3)
+    swift(3)
     spread_spectrum(filters[0] * land_forward(2) - spectrum[...])
     inverse(4)
 

time: 33.9 us -> 32.6 us (0.962)
  Pallas kernels: 32.4 us -> 31.1 us
    pallas_call x1, Pallas kernels: 32.4 us -> 31.1 us  [on_device_fused(): pl.pallas_call(functools.partial(section_kernel, rows, cols), out_shape=j...]
where the time goes in v4:
time: 32.6 us; the launch traced here: 32.5 us
  Pallas kernels  31.1 us (95%)
  other arithmetic  0.72 us (2%)
  between operations  0.64 us (2%)
    pallas_call x1, Pallas kernels, on_device_fused(): pl.pallas_call(functools.partial(section_kernel, rows, cols), out_shape=j...  31.1 us
    mul x1, other arithmetic, on_device_fused(): return (sections[0] * normalize + constant, sections[1] * normalize)  0.72 us

profile of v4, /device:TPU:0, one launch (start us, length us, event | category | flops | bytes accessed | tf_op | source)
XLA Modules:
  0.0 32.5 jit_solution(17331650744523249692)
XLA Ops:
  0.6 31.1 %shard_map.50 = f32[2,128,256]{2,1,0:T(8,128)S(1)} custom-call(f32[128,256]{1,0:T(8,128)} %u_hbm.1, f32[128,256]{1,0:T(8,128)} %v_hbm.1, f32[10,32,512]{2,1,0:T(8,128)} %constant.6.clone.tables_hbm), custom_call_target="tpu_custom_call" | custom-call | tf_op jit(solution)/shard_map/pallas_call | solution.py:499
  31.7 0.7 %multiply_bitcast_fusion = (f32[128,256]{1,0:T(8,128)}, f32[128,256]{1,0:T(8,128)}) fusion(f32[2,128,256]{2,1,0:T(8,128)S(1)} %shard_map.50), kind=kLoop, calls=%fused_computation | loop fusion | flops 98304 | bytes 524288 | tf_op jit(solution)/shard_map/mul | solution.py:534

commit v5 on v4

--- a/solution.py
+++ b/solution.py
@@ -206,7 +206,7 @@
     for step in range(1, cols):
         greet(barrier, row, lax.rem(col + step, cols))
     for step in range(1, rows):
-        greet(barrier, lax.rem(row + step, rows), col)
+        greet(barrier, lax.rem(row + rows - step, rows), col)
     pl.semaphore_wait(barrier, rows + cols - 2)
 
     def in_copy(step, field):
@@ -269,8 +269,8 @@
             dst_ref=recv.at[leg, me],
             send_sem=s_send.at[0],
             recv_sem=s_recv.at[leg],
-            device_id=(other // cols, lax.rem(other, cols)),
-            device_id_type=MESH,
+            device_id=other,
+            device_id_type=pl.DeviceIdType.LOGICAL,
         )
 
     def all_of(source, target, send_sem, recv_sem):

time: 32.6 us -> 32.6 us (level)
  no operation moved by 1% of the time
where the time goes in v5:
time: 32.6 us; the launch traced here: 32.5 us
  Pallas kernels  31.1 us (95%)
  other arithmetic  0.72 us (2%)
  between operations  0.64 us (2%)
    pallas_call x1, Pallas kernels, on_device_fused(): pl.pallas_call(functools.partial(section_kernel, rows, cols), out_shape=j...  31.1 us
    mul x1, other arithmetic, on_device_fused(): return (sections[0] * normalize + constant, sections[1] * normalize)  0.72 us

profile of v5, /device:TPU:0, one launch (start us, length us, event | category | flops | bytes accessed | tf_op | source)
XLA Modules:
  0.0 32.5 jit_solution(11064128704625352665)
XLA Ops:
  0.6 31.1 %shard_map.50 = f32[2,128,256]{2,1,0:T(8,128)S(1)} custom-call(f32[128,256]{1,0:T(8,128)} %u_hbm.1, f32[128,256]{1,0:T(8,128)} %v_hbm.1, f32[10,32,512]{2,1,0:T(8,128)} %constant.6.clone.tables_hbm), custom_call_target="tpu_custom_call" | custom-call | tf_op jit(solution)/shard_map/pallas_call | solution.py:499
  31.7 0.7 %multiply_bitcast_fusion = (f32[128,256]{1,0:T(8,128)}, f32[128,256]{1,0:T(8,128)}) fusion(f32[2,128,256]{2,1,0:T(8,128)S(1)} %shard_map.50), kind=kLoop, calls=%fused_computation | loop fusion | flops 98304 | bytes 524288 | tf_op jit(solution)/shard_map/mul | solution.py:534
